TPU v7x, 32 devices: a whole 2x2x4 slice. The times are simulated.
32 devices in a mesh: groups: 2 (over x), seq: 8 (over z, y), mp: 2 (over core).
Axes of the slice: x: 2, y: 2, z: 4, core: 2. Of those that a mesh axis runs over, the one named last changes fastest.
Arguments:
- latent_cache: bfloat16 [2048, 64, 512], P(('groups', 'seq')), parts along dimension 0, may hold values from -6 to 6
- rope_cache: bfloat16 [2048, 4096], P(('groups', 'seq')), parts along dimension 0, may hold values from -6 to 6
- q_nope: bfloat16 [16, 128, 128], P('groups', 'mp'), parts along dimension 0, may hold values from -12 to 12
- q_rope: bfloat16 [16, 128, 64], P('groups', 'mp'), parts along dimension 0, may hold values from -2000 to 2000
- w_uk: bfloat16 [128, 128, 512], P('mp', None, 'seq'), may hold values from -0.5 to 0.5
- value_up_weight: bfloat16 [128, 512, 128], P('mp', 'seq'), may hold values from -0.25 to 0.25
- w_out: bfloat16 [16384, 7168], P('mp', 'seq'), may hold values from -0.046875 to 0.046875
- page_table: int32 [16, 256], P('groups'), parts along dimension 0, may hold values from 0 to 1023, as said below
- lengths: int32 [16], P('groups'), parts along dimension 0, may hold values from 2048 to 16384, as said below
Outputs:
- output: bfloat16 [16, 7168], P('groups', ('seq', 'mp')), parts along dimension 0
There are 2 independent parts, one for each index of `groups`. A program takes and returns all parts, laid end to end along the dimension named above; an argument that names none is the same for every part. Nothing has to cross between parts.
Inputs may be any that keep to these rules, and one draw needn't show every extreme that they name: `lengths`: every sequence has one eighth of 16384 tokens or more; the longest has exactly 16384. page_table[b,p] for p < ceil(lengths[b] / 64) is the global slot (shard index times 128 plus local slot) holding that page; these live entries are all distinct; the other entries are 0 and unused.
All inputs are finite; a program needn't handle non-finite values.
Results may differ from a plain program's by a relative error of at most 0.012.
Values may be sent and summed in bfloat16 or wider, within the bound.
A program may use at most 128 MiB of HBM per device.

v0:
```python
import functools

import jax
import jax.numpy as jnp
from jax import lax
from jax.experimental import pallas as pl
from jax.experimental.pallas import tpu as pltpu
from jax.sharding import PartitionSpec as P

NEG = -1e30
MESH = pl.DeviceIdType.MESH
GROUP = 8
F32 = jnp.float32
BF16 = jnp.bfloat16


def greet(n, me, partner=None):
    barrier = pltpu.get_barrier_semaphore()
    for k in range(1, n):
        peer = lax.rem(me + k, n)
        pl.semaphore_signal(barrier, inc=1, device_id={"seq": peer}, device_id_type=MESH)
    if partner is not None:
        pl.semaphore_signal(barrier, inc=1, device_id={"mp": partner}, device_id_type=MESH)
    pl.semaphore_wait(barrier, n - 1 + (partner is not None))


def push(n, me, src_of, dst, send, recv):
    copies = []
    for k in range(1, n):
        peer = lax.rem(me + k, n)
        copy = pltpu.make_async_remote_copy(
            src_ref=src_of(peer), dst_ref=dst.at[me], send_sem=send.at[k], recv_sem=recv.at[k],
            device_id={"seq": peer}, device_id_type=MESH,
        )
        copy.start()
        copies.append(copy)
    return copies


def make_plan(first_slot, page, most, lengths_ref, table_ref, plan_ref):
    seqs, pages = table_ref.shape
    slots_dev, wide = most
    table = table_ref[...].astype(F32).T
    logical = lax.broadcasted_iota(jnp.int32, (pages, 1), 0)
    slot = lax.broadcasted_iota(jnp.int32, (pages, slots_dev), 1) + first_slot
    slot = slot.astype(F32)
    fill = []
    for b in range(seqs):
        inside = jnp.clip(lengths_ref[b] - page * logical, 0, page)
        hit = table[:, b:b + 1] == slot
        fill.append(jnp.sum(jnp.where(hit, inside, 0), axis=0, keepdims=True))
    eye = (lax.broadcasted_iota(jnp.int32, (slots_dev, slots_dev), 0)
           == lax.broadcasted_iota(jnp.int32, (slots_dev, slots_dev), 1))
    earlier = (lax.broadcasted_iota(jnp.int32, (slots_dev, slots_dev), 1)
               < lax.broadcasted_iota(jnp.int32, (slots_dev, slots_dev), 0))
    at = lax.broadcasted_iota(jnp.int32, (1, wide), 1)
    start = jnp.zeros((1, 1), jnp.int32)
    owner = jnp.zeros((1, wide), jnp.int32)
    target = jnp.full((slots_dev, 1), -1, jnp.int32)
    column = jnp.zeros((slots_dev, 1), jnp.int32)
    for b in range(seqs):
        owned = fill[b] > 0
        count = jnp.sum(owned.astype(jnp.int32), axis=1, keepdims=True)
        place = jnp.sum(jnp.where(earlier & owned, 1, 0), axis=1, keepdims=True)
        mine = jnp.sum(jnp.where(eye, fill[b], 0), axis=1, keepdims=True)
        target = jnp.where(mine > 0, start * GROUP + place, target)
        column = column + mine
        start = start + (count + GROUP - 1) // GROUP
        owner = owner + (at >= start).astype(jnp.int32)
    match = target == lax.broadcasted_iota(jnp.int32, (slots_dev, wide), 1)
    ids = lax.broadcasted_iota(jnp.int32, (slots_dev, wide), 0)
    plan_ref[0:1, :] = jnp.sum(jnp.where(match, ids, 0), axis=0, keepdims=True)
    plan_ref[1:2, :] = jnp.sum(jnp.where(match, column, 0), axis=0, keepdims=True)
    plan_ref[2:3, :] = jnp.minimum(owner, seqs - 1)
    plan_ref[3:4, :] = jnp.broadcast_to(start, (1, wide))
    plan_ref[4:8, :] = jnp.zeros((4, wide), jnp.int32)


def query_kernel(n, pack, page, lengths_ref, table_ref, rope_ref, q_ref, w_ref, out_ref, plan_ref, spread_ref,
                 raw, flat, gath, wide_rope, send, recv, send2, recv2):
    me = lax.axis_index("seq")
    seqs, heads, _ = q_ref.shape
    cols = w_ref.shape[1]
    partner = me + 1 - 2 * lax.rem(me, 2)
    barrier = pltpu.get_barrier_semaphore()
    for peer in [lax.rem(me + 2 * k, n) for k in range(1, n // 2)] + [partner]:
        pl.semaphore_signal(barrier, inc=1, device_id={"seq": peer}, device_id_type=MESH)
    for b in range(seqs):
        flat[b * heads:(b + 1) * heads, :] = q_ref[b].astype(F32)
    for h in range(heads):
        q = flat[pl.ds(h, seqs, stride=heads), :].astype(BF16)
        raw[h * seqs:(h + 1) * seqs, :] = lax.dot_general(
            q, w_ref[h], (((1,), (1,)), ((), ())), preferred_element_type=F32)
    for b in range(0, seqs, pack):
        parts = [raw[pl.ds(b + j, heads, stride=seqs), :] for j in range(pack)]
        row = parts[0] if pack == 1 else jnp.concatenate(parts, axis=1)
        gath[me, b // pack * heads:(b // pack + 1) * heads, :] = row.astype(BF16)
    pl.semaphore_wait(barrier, n // 2)

    def send_to(block, peer, s, r):
        copy = pltpu.make_async_remote_copy(
            src_ref=gath.at[block], dst_ref=gath.at[block], send_sem=s, recv_sem=r,
            device_id={"seq": peer}, device_id_type=MESH)
        copy.start()
        return copy

    across = [send_to(me, partner, send2.at[0], recv2.at[0])]
    line = [send_to(me, lax.rem(me + 2 * k, n), send.at[k], recv.at[k]) for k in range(1, n // 2)]

    slots_dev = rope_ref.shape[0]
    make_plan(me * slots_dev, page, (slots_dev, plan_ref.shape[1]), lengths_ref, table_ref, plan_ref)
    per = page * 128 // rope_ref.shape[1]
    lane = lax.broadcasted_iota(jnp.int32, (slots_dev, 128), 1) // (128 // per)
    for i in range(rope_ref.shape[1] // 128):
        x = rope_ref[:, i * 128:(i + 1) * 128].astype(F32)
        for j in range(per):
            wide_rope[pl.ds(i * per + j, slots_dev, stride=page), :] = jnp.where(lane == j, x, 0.0)

    def narrow(i, _):
        spread_ref[i] = wide_rope[pl.ds(pl.multiple_of(i * page, page), page), :].astype(BF16)
        return 0

    lax.fori_loop(0, slots_dev, narrow, 0, unroll=4)

    for k in range(1, n // 2):
        line[k - 1].wait_recv()
        across.append(send_to(lax.rem(me - 2 * k + n, n), partner, send2.at[k], recv2.at[k]))
    for copy in line:
        copy.wait_send()
    for copy in across:
        copy.wait()
    for s in range(n):
        for b in range(seqs):
            at = b % pack * cols
            out_ref[b, :, s * cols:(s + 1) * cols] = gath[
                s, b // pack * heads:(b // pack + 1) * heads, at:at + cols]


def attend_kernel(scale, pack, plan_ref, q_ref, qr_ref, rope_ref, latent_ref,
                  out_ref, kbuf, acc, top, total, sems):
    seqs, heads, width = q_ref.shape
    page = latent_ref.shape[1]
    tokens = GROUP * page
    n = out_ref.shape[0]
    cols = width // n
    count = plan_ref[3, 0]
    acc[...] = jnp.zeros_like(acc)
    top[...] = jnp.full(top.shape, NEG, F32)
    total[...] = jnp.zeros_like(total)

    def fetch(c, buf):
        return [pltpu.make_async_copy(
            latent_ref.at[plan_ref[0, c * GROUP + g]], kbuf.at[buf, pl.ds(g * page, page)], sems.at[buf, g])
            for g in range(GROUP)]

    for ahead in range(2):
        @pl.when(count > ahead)
        def _():
            for copy in fetch(ahead, ahead):
                copy.start()

    lane = lax.broadcasted_iota(jnp.int32, (1, tokens), 1)

    def step(c, _):
        buf = lax.rem(c, 3)

        @pl.when(c + 2 < count)
        def _():
            for copy in fetch(c + 2, lax.rem(c + 2, 3)):
                copy.start()

        b = plan_ref[2, c]
        rope = jnp.concatenate([rope_ref[plan_ref[0, c * GROUP + g]] for g in range(GROUP)], axis=0)
        limit = jnp.zeros((1, tokens), jnp.int32)
        for g in range(GROUP):
            limit = jnp.where(lane // page == g, plan_ref[1, c * GROUP + g] + g * page, limit)
        nt = (((1,), (1,)), ((), ()))
        score = lax.dot_general(qr_ref[b], rope, nt, preferred_element_type=F32)
        for copy in fetch(c, buf):
            copy.wait()
        keys = kbuf[buf]
        score = (score + lax.dot_general(q_ref[b], keys, nt, preferred_element_type=F32)) * scale
        score = jnp.where(lane < limit, score, NEG)
        old = top[b][:, :1]
        new = jnp.maximum(old, jnp.max(score, axis=1, keepdims=True))
        weight = jnp.exp(score - new)
        carry = jnp.exp(old - new)
        total[b] = total[b] * carry + jnp.sum(weight, axis=1, keepdims=True)
        top[b] = jnp.broadcast_to(new, top.shape[1:])
        acc[b] = acc[b] * carry + jnp.dot(weight.astype(BF16), keys, preferred_element_type=F32)
        return 0

    lax.fori_loop(0, count, step, 0)

    ids = lax.broadcasted_iota(jnp.int32, (heads, 128), 1)
    extra = jnp.zeros((heads, 128), F32)
    for b in range(seqs):
        inv = 1.0 / jnp.maximum(total[b][:, :1], 1e-30)
        whole = acc[b] * inv
        for s in range(n):
            at = b % pack * cols
            out_ref[s, b // pack * heads:(b // pack + 1) * heads, at:at + cols] = whole[
                :, s * cols:(s + 1) * cols].astype(BF16)
        for k, value in enumerate((top[b], total[b])):
            for j in range(3):
                term = value.astype(BF16).astype(F32)
                extra = jnp.where(ids == (k * 3 + j) * seqs + b, term, extra)
                value = value - term
    base = seqs // pack * heads
    lanes = out_ref.shape[2]
    for s in range(n):
        out_ref[s, base:base + heads, :] = extra[:, :lanes].astype(BF16)


def finish_kernel(n, pack, o_ref, v_ref, w_hbm, out_ref, gath, port, pv, part, vals, lhs, w_buf, res,
                  tx, rx, send1, recv1, send2, recv2, send3, recv3, send4, recv4, wsem):
    me = lax.axis_index("seq")
    half = lax.axis_index("mp")
    heads, cols, vdim = v_ref.shape
    seqs = lhs.shape[0]
    hs = heads // n
    load = pltpu.make_async_copy(w_hbm, w_buf, wsem)
    load.start()
    greet(n, me, 1 - half)
    copies = push(n, me, lambda peer: o_ref.at[peer], gath, send1, recv1)
    gath[me] = o_ref[me]
    for copy in copies:
        copy.wait()

    base = seqs // pack * heads
    tops, sums = [], []
    for s in range(n):
        e = gath[s, base:base + heads, :].astype(F32)
        terms = [e[:, k * seqs:(k + 1) * seqs] for k in range(6)]
        tops.append(terms[0] + terms[1] + terms[2])
        sums.append(terms[3] + terms[4] + terms[5])
    best = functools.reduce(jnp.maximum, tops)
    shares = [x * jnp.exp(t - best) for t, x in zip(tops, sums)]
    inv = 1.0 / functools.reduce(jnp.add, shares)
    shares = [x * inv for x in shares]
    lane = lax.broadcasted_iota(jnp.int32, (heads, pack * cols), 1) // cols
    for p in range(seqs // pack):
        total = jnp.zeros((heads, pack * cols), F32)
        for s in range(n):
            share = jnp.broadcast_to(shares[s][:, p * pack:p * pack + 1], total.shape)
            for j in range(1, pack):
                share = jnp.where(lane == j, shares[s][:, p * pack + j:p * pack + j + 1], share)
            total = total + gath[s, p * heads:(p + 1) * heads, :].astype(F32) * share
        for j in range(pack):
            b = p * pack + j
            port[b * heads:(b + 1) * heads, :] = total[:, j * cols:(j + 1) * cols]
    for h in range(heads):
        x = port[pl.ds(h, seqs, stride=heads), :].astype(BF16)
        pv[h // hs, h % hs * seqs:(h % hs + 1) * seqs, :] = jnp.dot(
            x, v_ref[h], preferred_element_type=F32).astype(BF16)
    copies = push(n, me, lambda peer: pv.at[peer], part, send2, recv2)
    part[me] = pv[me]
    for copy in copies:
        copy.wait()
    total = part[0].astype(F32)
    for s in range(1, n):
        total = total + part[s].astype(F32)
    vals[me] = total.astype(BF16)
    copies = push(n, me, lambda peer: vals.at[me], vals, send3, recv3)
    for copy in copies:
        copy.wait()
    for h in range(heads):
        lhs[:, h * vdim:(h + 1) * vdim] = vals[h // hs, h % hs * seqs:(h % hs + 1) * seqs, :]
    load.wait()
    rows = w_buf.shape[0]
    res[...] = jnp.zeros_like(res)
    cut = 1024

    def body(i, _):
        at = pl.ds(pl.multiple_of(i * cut, cut), cut)
        res[...] += jnp.dot(lhs[:, at], w_buf[at, :], preferred_element_type=F32)
        return 0

    lax.fori_loop(0, rows // cut, body, 0)
    wide = res.shape[1] // 2
    low, high = res[:, :wide], res[:, wide:]
    first = half == 0
    tx[...] = jnp.where(first, high, low)
    copy = pltpu.make_async_remote_copy(
        src_ref=tx, dst_ref=rx, send_sem=send4, recv_sem=recv4,
        device_id={"mp": 1 - half}, device_id_type=MESH)
    copy.start()
    copy.wait()
    out_ref[...] = (jnp.where(first, low, high) + rx[...]).astype(BF16)


def local(n, latent_cache, rope_cache, q_nope, q_rope, w_uk, value_up_weight, w_out, page_table, lengths):
    slots_dev, page, width = latent_cache.shape
    seqs, heads, nope = q_nope.shape
    rope_w = q_rope.shape[2]
    cols = w_uk.shape[2]
    vdim = value_up_weight.shape[2]
    scale = (nope + rope_w) ** (-0.5)
    pack = max(1, min(seqs, 128 // cols))
    lanes = pack * cols
    vm = pl.BlockSpec(memory_space=pltpu.VMEM)
    sm = pl.BlockSpec(memory_space=pltpu.SMEM)
    hbm = pl.BlockSpec(memory_space=pl.ANY)
    dma = pltpu.SemaphoreType.DMA
    params = functools.partial(pltpu.CompilerParams, has_side_effects=True)

    most = (slots_dev + seqs * (GROUP - 1)) // GROUP * GROUP
    per = 128 // rope_w
    q_latent, steps, rope = pl.pallas_call(
        functools.partial(query_kernel, n, pack, page),
        out_shape=(
            jax.ShapeDtypeStruct((seqs, heads, width), BF16),
            jax.ShapeDtypeStruct((8, (most + 127) // 128 * 128), jnp.int32),
            jax.ShapeDtypeStruct((slots_dev, page, 128), BF16),
        ),
        in_specs=[sm, vm, vm, vm, vm], out_specs=(vm, vm, vm),
        scratch_shapes=[
            pltpu.VMEM((heads * seqs, cols), F32),
            pltpu.VMEM((heads * seqs, nope), F32),
            pltpu.VMEM((n, seqs // pack * heads, lanes), BF16),
            pltpu.VMEM((slots_dev * page, 128), F32),
            dma((n // 2,)), dma((n // 2,)), dma((n // 2,)), dma((n // 2,)),
        ],
        compiler_params=params(collective_id=1), name="queries",
    )(lengths, page_table, rope_cache, q_nope, w_uk.transpose(0, 2, 1))

    rows = seqs // pack * heads + heads
    mixed = pl.pallas_call(
        functools.partial(attend_kernel, scale, pack),
        out_shape=jax.ShapeDtypeStruct((n, rows, lanes), BF16),
        in_specs=[sm, vm, vm, vm, hbm], out_specs=vm,
        scratch_shapes=[
            pltpu.VMEM((3, GROUP * page, width), BF16),
            pltpu.VMEM((seqs, heads, width), F32),
            pltpu.VMEM((seqs, heads, 128), F32),
            pltpu.VMEM((seqs, heads, 128), F32),
            dma((3, GROUP)),
        ],
        name="attend",
    )(steps, q_latent, jnp.concatenate([q_rope] * per, axis=2), rope, latent_cache)

    wide = w_out.shape[1]
    hs = heads // n
    return pl.pallas_call(
        functools.partial(finish_kernel, n, pack),
        out_shape=jax.ShapeDtypeStruct((seqs, wide // 2), BF16),
        in_specs=[vm, vm, hbm], out_specs=vm,
        scratch_shapes=[
            pltpu.VMEM((n, rows, lanes), BF16),
            pltpu.VMEM((seqs * heads, cols), F32),
            pltpu.VMEM((n, hs * seqs, vdim), BF16),
            pltpu.VMEM((n, hs * seqs, vdim), BF16),
            pltpu.VMEM((n, hs * seqs, vdim), BF16),
            pltpu.VMEM((seqs, heads * vdim), BF16),
            pltpu.VMEM(w_out.shape, BF16),
            pltpu.VMEM((seqs, wide), F32),
            pltpu.VMEM((seqs, wide // 2), F32),
            pltpu.VMEM((seqs, wide // 2), F32),
            dma((n,)), dma((n,)), dma((n,)), dma((n,)), dma((n,)), dma((n,)), dma, dma, dma,
        ],
        compiler_params=params(collective_id=2, vmem_limit_bytes=48 * 1024 * 1024), name="finish",
    )(mixed, value_up_weight, w_out)


def solution(mesh):
    return jax.shard_map(
        functools.partial(local, mesh.shape["seq"]),
        mesh=mesh,
        in_specs=(
            P(("groups", "seq"), None, None),
            P(("groups", "seq"), None),
            P("groups", "mp", None),
            P("groups", "mp", None),
            P("mp", None, "seq"),
            P("mp", "seq", None),
            P("mp", "seq"),
            P("groups", None),
            P("groups"),
        ),
        out_specs=P("groups", ("seq", "mp")),
        check_vma=False,
    )
```

profile of v0, /device:TPU:0, one launch (start us, length us, event | category | flops | bytes accessed | tf_op | source)
XLA Modules:
  0.0 74.5 jit_solution(16380042291715989152)
XLA Ops:
  0.0 0.0 copy-start.1
  0.0 1.8 %pad_maximum_fusion.qr_ref = bf16[8,64,128]{2,1,0:T(8,128)(2,1)} fusion(bf16[8,64,64]{2,1,0:T(8,128)(2,1)} %param.12), kind=kLoop, calls=%fused_computation | loop fusion | flops 262144 | bytes 196608 | tf_op jit(solution)/shard_map/concatenate | solution.py:340
  1.8 20.2 %queries.1 = (bf16[8,64,512]{2,1,0:T(8,128)(2,1)}, s32[8,256]{1,0:T(8,128)}, bf16[128,64,128]{2,1,0:T(8,128)(2,1)}) custom-call(s32[8]{0:T(128)} %lengths_ref.1, s32[8,256]{1,0:T(8,128)} %table_ref.1, bf16[128,4096]{1,0:T(8,128)(2,1)} %rope_ref.1, bf16[8,64,128]{2,1,0:T(8,128)(2,1)} %q_ref.1, bf16[64,64,128]{2,1,0:T(8,128)(2,1)} %bitcast.1), custom_call_target="tpu_custom_call" | custom-call | tf_op jit(solution)/shard_map/queries/pallas_call | solution.py:309
  22.1 6.3 %attend.1.o_ref = bf16[8,320,128]{2,1,0:T(8,128)(2,1)} custom-call(s32[8,256]{1,0:T(8,128)} %get-tuple-element.8.plan_ref, bf16[8,64,512]{2,1,0:T(8,128)(2,1)} %get-tuple-element.9.q_ref, bf16[8,64,128]{2,1,0:T(8,128)(2,1)} %pad_maximum_fusion.qr_ref, bf16[128,64,128]{2,1,0:T(8,128)(2,1)} %get-tuple-element.10.rope_ref, bf16[128,64,512]{2,1,0:T(8,128)(2,1)} %latent_ref.1), custom_call_target="tpu_custom_call" | custom-call | tf_op jit(solution)/shard_map/attend/pallas_call | solution.py:328
  28.4 0.0 copy-done.1
  28.4 0.0 copy-start
  28.4 1.1 %copy-done = bf16[8,320,128]{2,1,0:T(8,128)(2,1)S(1)} copy-done((bf16[8,320,128]{2,1,0:T(8,128)(2,1)S(1)}, bf16[8,320,128]{2,1,0:T(8,128)(2,1)}, u32[]{:S(2)}) %copy-start) | copy-done | bytes 655384
  29.5 44.4 %finish.1 = bf16[8,448]{1,0:T(8,128)(2,1)S(1)} custom-call(bf16[8,320,128]{2,1,0:T(8,128)(2,1)S(1)} %copy-done, bf16[64,64,128]{2,1,0:T(8,128)(2,1)S(1)} %copy-done.1, bf16[8192,896]{1,0:T(8,128)(2,1)} %w_hbm.1), custom_call_target="tpu_custom_call" | custom-call | tf_op jit(solution)/shard_map/finish/pallas_call | solution.py:344
  73.9 0.6 copy.11
Async XLA Ops:
  0.0 28.4 %copy-start.1 = (bf16[64,64,128]{2,1,0:T(8,128)(2,1)S(1)}, bf16[64,64,128]{2,1,0:T(8,128)(2,1)}, u32[]{:S(2)}) copy-start(bf16[64,64,128]{2,1,0:T(8,128)(2,1)} %v_ref.1) | copy-start | bytes 3145732
  28.4 1.1 %copy-start = (bf16[8,320,128]{2,1,0:T(8,128)(2,1)S(1)}, bf16[8,320,128]{2,1,0:T(8,128)(2,1)}, u32[]{:S(2)}) copy-start(bf16[8,320,128]{2,1,0:T(8,128)(2,1)} %attend.1.o_ref) | copy-start | bytes 1966084
where the time goes:
time: 74.9 us; the launch traced here: 74.5 us
  Pallas kernels  70.9 us (95%)
  other arithmetic  1.82 us (2%)
  local copies, waits for them, and re-layouts  1.69 us (2%)
    pallas_call x1, Pallas kernels, local(): pl.pallas_call(functools.partial(finish_kernel, n, pack), out_shape=jax.S...  44.4 us
    pallas_call x1, Pallas kernels, local(): pl.pallas_call(functools.partial(query_kernel, n, pack, page), out_shape=...  20.2 us
    pallas_call x1, Pallas kernels, local(): pl.pallas_call(functools.partial(attend_kernel, scale, pack), out_shape=j...  6.29 us
    concatenate x1, other arithmetic, local(): jnp.concatenate([q_rope] * per, axis=2)  1.82 us
    unnamed x5, local copies, waits for them, and re-layouts  1.69 us

commit v1 on v0

--- a/solution.py
+++ b/solution.py
@@ -137,7 +137,7 @@
 
 
 def attend_kernel(scale, pack, plan_ref, q_ref, qr_ref, rope_ref, latent_ref,
-                  out_ref, kbuf, acc, top, total, sems):
+                  out_ref, kbuf, acc, top, total, turn, ready, sems):
     seqs, heads, width = q_ref.shape
     page = latent_ref.shape[1]
     tokens = GROUP * page
@@ -153,7 +153,7 @@
             latent_ref.at[plan_ref[0, c * GROUP + g]], kbuf.at[buf, pl.ds(g * page, page)], sems.at[buf, g])
             for g in range(GROUP)]
 
-    for ahead in range(2):
+    for ahead in range(3):
         @pl.when(count > ahead)
         def _():
             for copy in fetch(ahead, ahead):
@@ -161,33 +161,51 @@
 
     lane = lax.broadcasted_iota(jnp.int32, (1, tokens), 1)
 
-    def step(c, _):
-        buf = lax.rem(c, 3)
-
-        @pl.when(c + 2 < count)
-        def _():
-            for copy in fetch(c + 2, lax.rem(c + 2, 3)):
-                copy.start()
-
+    for b in range(seqs):
+        turn[b] = jnp.concatenate([qr_ref[b]] * (128 // qr_ref.shape[2]), axis=1)
+
+    def score_of(c):
         b = plan_ref[2, c]
         rope = jnp.concatenate([rope_ref[plan_ref[0, c * GROUP + g]] for g in range(GROUP)], axis=0)
         limit = jnp.zeros((1, tokens), jnp.int32)
         for g in range(GROUP):
             limit = jnp.where(lane // page == g, plan_ref[1, c * GROUP + g] + g * page, limit)
         nt = (((1,), (1,)), ((), ()))
-        score = lax.dot_general(qr_ref[b], rope, nt, preferred_element_type=F32)
-        for copy in fetch(c, buf):
+        score = lax.dot_general(turn[b], rope, nt, preferred_element_type=F32)
+        keys = kbuf[lax.rem(c, 4)]
+        score = (score + lax.dot_general(q_ref[b], keys, nt, preferred_element_type=F32)) * scale
+        return jnp.where(lane < limit, score, NEG)
+
+    @pl.when(count > 0)
+    def _():
+        for copy in fetch(0, 0):
             copy.wait()
-        keys = kbuf[buf]
-        score = (score + lax.dot_general(q_ref[b], keys, nt, preferred_element_type=F32)) * scale
-        score = jnp.where(lane < limit, score, NEG)
+        ready[...] = score_of(0)
+
+    def step(c, _):
+        @pl.when(c + 3 < count)
+        def _():
+            for copy in fetch(c + 3, lax.rem(c + 3, 4)):
+                copy.start()
+
+        @pl.when(c + 1 < count)
+        def _():
+            for copy in fetch(c + 1, lax.rem(c + 1, 4)):
+                copy.wait()
+
+        score = ready[...]
+        upcoming = score_of(c + 1)
+        b = plan_ref[2, c]
+        keys = kbuf[lax.rem(c, 4)]
         old = top[b][:, :1]
         new = jnp.maximum(old, jnp.max(score, axis=1, keepdims=True))
         weight = jnp.exp(score - new)
         carry = jnp.exp(old - new)
+        product = jnp.dot(weight.astype(BF16), keys, preferred_element_type=F32)
         total[b] = total[b] * carry + jnp.sum(weight, axis=1, keepdims=True)
         top[b] = jnp.broadcast_to(new, top.shape[1:])
-        acc[b] = acc[b] * carry + jnp.dot(weight.astype(BF16), keys, preferred_element_type=F32)
+        acc[b] = acc[b] * carry + product
+        ready[...] = upcoming
         return 0
 
     lax.fori_loop(0, count, step, 0)
@@ -262,21 +280,22 @@
         total = total + part[s].astype(F32)
     vals[me] = total.astype(BF16)
     copies = push(n, me, lambda peer: vals.at[me], vals, send3, recv3)
+    load.wait()
+    rows = hs * vdim
+    for k in range(n):
+        src = lax.rem(me - k + n, n)
+        if k:
+            copies[k - 1].wait_recv()
+        for h in range(hs):
+            lhs[:, h * vdim:(h + 1) * vdim] = vals[src, h * seqs:(h + 1) * seqs, :]
+        at = pl.ds(pl.multiple_of(src * rows, rows), rows)
+        product = jnp.dot(lhs[...], w_buf[at, :], preferred_element_type=F32)
+        if k:
+            res[...] += product
+        else:
+            res[...] = product
     for copy in copies:
-        copy.wait()
-    for h in range(heads):
-        lhs[:, h * vdim:(h + 1) * vdim] = vals[h // hs, h % hs * seqs:(h % hs + 1) * seqs, :]
-    load.wait()
-    rows = w_buf.shape[0]
-    res[...] = jnp.zeros_like(res)
-    cut = 1024
-
-    def body(i, _):
-        at = pl.ds(pl.multiple_of(i * cut, cut), cut)
-        res[...] += jnp.dot(lhs[:, at], w_buf[at, :], preferred_element_type=F32)
-        return 0
-
-    lax.fori_loop(0, rows // cut, body, 0)
+        copy.wait_send()
     wide = res.shape[1] // 2
     low, high = res[:, :wide], res[:, wide:]
     first = half == 0
@@ -305,12 +324,11 @@
     params = functools.partial(pltpu.CompilerParams, has_side_effects=True)
 
     most = (slots_dev + seqs * (GROUP - 1)) // GROUP * GROUP
-    per = 128 // rope_w
     q_latent, steps, rope = pl.pallas_call(
         functools.partial(query_kernel, n, pack, page),
         out_shape=(
             jax.ShapeDtypeStruct((seqs, heads, width), BF16),
-            jax.ShapeDtypeStruct((8, (most + 127) // 128 * 128), jnp.int32),
+            jax.ShapeDtypeStruct((8, (most + GROUP + 127) // 128 * 128), jnp.int32),
             jax.ShapeDtypeStruct((slots_dev, page, 128), BF16),
         ),
         in_specs=[sm, vm, vm, vm, vm], out_specs=(vm, vm, vm),
@@ -321,7 +339,7 @@
             pltpu.VMEM((slots_dev * page, 128), F32),
             dma((n // 2,)), dma((n // 2,)), dma((n // 2,)), dma((n // 2,)),
         ],
-        compiler_params=params(collective_id=1), name="queries",
+        compiler_params=params(collective_id=1, vmem_limit_bytes=58 * 1024 * 1024), name="queries",
     )(lengths, page_table, rope_cache, q_nope, w_uk.transpose(0, 2, 1))
 
     rows = seqs // pack * heads + heads
@@ -330,14 +348,17 @@
         out_shape=jax.ShapeDtypeStruct((n, rows, lanes), BF16),
         in_specs=[sm, vm, vm, vm, hbm], out_specs=vm,
         scratch_shapes=[
-            pltpu.VMEM((3, GROUP * page, width), BF16),
+            pltpu.VMEM((4, GROUP * page, width), BF16),
             pltpu.VMEM((seqs, heads, width), F32),
             pltpu.VMEM((seqs, heads, 128), F32),
             pltpu.VMEM((seqs, heads, 128), F32),
-            dma((3, GROUP)),
+            pltpu.VMEM((seqs, heads, 128), BF16),
+            pltpu.VMEM((heads, GROUP * page), F32),
+            dma((4, GROUP)),
         ],
+        compiler_params=pltpu.CompilerParams(vmem_limit_bytes=58 * 1024 * 1024),
         name="attend",
-    )(steps, q_latent, jnp.concatenate([q_rope] * per, axis=2), rope, latent_cache)
+    )(steps, q_latent, q_rope, rope, latent_cache)
 
     wide = w_out.shape[1]
     hs = heads // n
@@ -351,14 +372,14 @@
             pltpu.VMEM((n, hs * seqs, vdim), BF16),
             pltpu.VMEM((n, hs * seqs, vdim), BF16),
             pltpu.VMEM((n, hs * seqs, vdim), BF16),
-            pltpu.VMEM((seqs, heads * vdim), BF16),
+            pltpu.VMEM((seqs, hs * vdim), BF16),
             pltpu.VMEM(w_out.shape, BF16),
             pltpu.VMEM((seqs, wide), F32),
             pltpu.VMEM((seqs, wide // 2), F32),
             pltpu.VMEM((seqs, wide // 2), F32),
             dma((n,)), dma((n,)), dma((n,)), dma((n,)), dma((n,)), dma((n,)), dma, dma, dma,
         ],
-        compiler_params=params(collective_id=2, vmem_limit_bytes=48 * 1024 * 1024), name="finish",
+        compiler_params=params(collective_id=2, vmem_limit_bytes=58 * 1024 * 1024), name="finish",
     )(mixed, value_up_weight, w_out)
 
 

time: 74.9 us -> 69.8 us (0.932)
  Pallas kernels: 70.9 us -> 67.5 us
  other arithmetic: 1.82 us -> 0 us
    pallas_call x1, Pallas kernels: 44.4 us -> 40 us  [local(): pl.pallas_call(functools.partial(finish_kernel, n, pack), out_shape=jax.S...]
    concatenate x1 -> x0, other arithmetic: 1.82 us -> none  [local(): jnp.concatenate([q_rope] * per, axis=2)]
    pallas_call x1, Pallas kernels: 6.29 us -> 7.27 us  [local(): pl.pallas_call(functools.partial(attend_kernel, scale, pack), out_shape=j...]
    unnamed x5 -> x1, local copies, waits for them, and re-layouts: 1.69 us -> 1.3 us
where the time goes in v1:
time: 69.8 us; the launch traced here: 68.8 us
  Pallas kernels  67.5 us (97%)
  local copies, waits for them, and re-layouts  1.3 us (2%)
    pallas_call x1, Pallas kernels, local(): pl.pallas_call(functools.partial(finish_kernel, n, pack), out_shape=jax.S...  40 us
    pallas_call x1, Pallas kernels, local(): pl.pallas_call(functools.partial(query_kernel, n, pack, page), out_shape=...  20.2 us
    pallas_call x1, Pallas kernels, local(): pl.pallas_call(functools.partial(attend_kernel, scale, pack), out_shape=j...  7.27 us

profile of v1, /device:TPU:0, one launch (start us, length us, event | category | flops | bytes accessed | tf_op | source)
XLA Modules:
  0.0 68.8 jit_solution(7909092339813670737)
XLA Ops:
  0.0 20.2 %queries.1 = (bf16[8,64,512]{2,1,0:T(8,128)(2,1)}, s32[8,256]{1,0:T(8,128)}, bf16[128,64,128]{2,1,0:T(8,128)(2,1)}) custom-call(s32[8]{0:T(128)} %lengths_ref.1, s32[8,256]{1,0:T(8,128)} %table_ref.1, bf16[128,4096]{1,0:T(8,128)(2,1)} %rope_ref.1, bf16[8,64,128]{2,1,0:T(8,128)(2,1)} %q_ref.1, bf16[64,64,128]{2,1,0:T(8,128)(2,1)} %bitcast.1), custom_call_target="tpu_custom_call" | custom-call | tf_op jit(solution)/shard_map/queries/pallas_call | solution.py:327
  20.2 7.3 %attend.1.o_ref = bf16[8,320,128]{2,1,0:T(8,128)(2,1)} custom-call(s32[8,256]{1,0:T(8,128)} %get-tuple-element.8.plan_ref, bf16[8,64,512]{2,1,0:T(8,128)(2,1)} %get-tuple-element.9.q_ref, bf16[8,64,64]{2,1,0:T(8,128)(2,1)} %qr_ref.1, bf16[128,64,128]{2,1,0:T(8,128)(2,1)} %get-tuple-element.10.rope_ref, bf16[128,64,512]{2,1,0:T(8,128)(2,1)} %latent_ref.1), custom_call_target="tpu_custom_call" | custom-call | tf_op jit(solution)/shard_map/attend/pallas_call | solution.py:346
  27.5 40.0 %finish.1 = bf16[8,448]{1,0:T(8,128)(2,1)} custom-call(bf16[8,320,128]{2,1,0:T(8,128)(2,1)} %attend.1.o_ref, bf16[64,64,128]{2,1,0:T(8,128)(2,1)} %v_ref.1, bf16[8192,896]{1,0:T(8,128)(2,1)} %w_hbm.1), custom_call_target="tpu_custom_call" | custom-call | tf_op jit(solution)/shard_map/finish/pallas_call | solution.py:365
  67.5 1.3 %copy.11 = bf16[8,448]{1,0:T(8,128)(2,1)} copy(bf16[8,448]{1,0:T(8,128)(2,1)} %finish.1) | data formatting | bytes 14336
